TPU v7x, 32 devices: a whole 2x2x4 slice. The times are simulated.
32 devices in a mesh: lon: 8 (over z, y), day: 4 (over x, core).
Axes of the slice: x: 2, y: 2, z: 4, core: 2. Of those that a mesh axis runs over, the one named last changes fastest.
Arguments:
- field: bfloat16 [92, 720, 1024], P('day', 'lon'), may hold values from -6 to 6
Outputs:
- filtered: float32 [92, 720, 1024], P('day', 'lon')
All inputs are finite; a program needn't handle non-finite values.
Results may differ from a plain program's by a relative error of at most 0.0003.
Values may be sent and summed in bfloat16 or wider, within the bound.
A program may use at most 192 MiB of HBM per device.

v0:
```python
import jax
import jax.numpy as jnp
from jax import lax
from jax.sharding import PartitionSpec as P

DAY_HALF = 15
LON_HALF = 10


def extended_2(cells, sides, width):
    for axis, dim in sides:
        count = lax.axis_size(axis)
        head = lax.slice_in_dim(cells, 0, width, axis=dim)
        tail = lax.slice_in_dim(cells, cells.shape[dim] - width, cells.shape[dim], axis=dim)
        cells = jnp.concatenate(
            [
                lax.ppermute(tail, axis, [(i, (i + 1) % count) for i in range(count)]),
                cells,
                lax.ppermute(head, axis, [((i + 1) % count, i) for i in range(count)]),
            ],
            axis=dim,
        )
    return cells


def running(values, dim, half):
    count = values.shape[dim] - 2 * half
    total = jnp.cumsum(values, axis=dim)
    first = jnp.zeros_like(lax.slice_in_dim(total, 0, 1, axis=dim))
    total = jnp.concatenate([first, total], axis=dim)
    upper = lax.slice_in_dim(total, 2 * half + 1, 2 * half + 1 + count, axis=dim)
    lower = lax.slice_in_dim(total, 0, count, axis=dim)
    return (upper - lower) / (2.0 * half + 1.0)


def local(field):
    widened = extended_2(field, (("lon", 1),), LON_HALF)
    extended = extended_2(widened, (("day", 0),), DAY_HALF)
    values = extended.astype(jnp.float32)
    clim = running(values, 0, DAY_HALF)
    anomaly = values[DAY_HALF : values.shape[0] - DAY_HALF] - clim
    return running(anomaly, 1, LON_HALF)


def solution(mesh):
    return jax.shard_map(
        local,
        mesh=mesh,
        in_specs=(P("day", "lon", None),),
        out_specs=P("day", "lon", None),
        check_vma=False,
    )
```

profile of v0, /device:TPU:0, one launch (start us, length us, event | category | flops | bytes accessed | tf_op | source)
XLA Modules:
  0.0 167.7 jit_solution(17313164957506284362)
XLA Ops:
  0.0 1.2 fusion.9
  1.2 3.0 %collective-permute-start = (bf16[23,10,1024]{2,0,1:T(8,128)(2,1)S(1)}, bf16[23,10,1024]{2,0,1:T(8,128)(2,1)S(1)}, u32[]{:S(2)}, u32[]{:S(2)}) collective-permute-start(bf16[23,10,1024]{2,0,1:T(8,128)(2,1)S(1)} %get-tuple-element.7), channel_id=1, source_target_pairs={{0,4},{4,8},{8,12},{12,16},{16,20},{20,24},{24,28},{28,0},{1,5},{5... | collective-permute-start | bytes 1413128 | tf_op jit(solution)/shard_map/ppermute | solution.py:17
  4.3 3.1 %collective-permute-start.1 = (bf16[23,10,1024]{2,0,1:T(8,128)(2,1)S(1)}, bf16[23,10,1024]{2,0,1:T(8,128)(2,1)S(1)}, u32[]{:S(2)}, u32[]{:S(2)}) collective-permute-start(bf16[23,10,1024]{2,0,1:T(8,128)(2,1)S(1)} %get-tuple-element.8), channel_id=1, source_target_pairs={{4,0},{8,4},{12,8},{16,12},{20,16},{24,20},{28,24},{0,28},{5,1},{9... | collective-permute-start | bytes 1413128 | tf_op jit(solution)/shard_map/ppermute | solution.py:19
  7.4 4.7 %copy.7 = bf16[23,90,1024]{2,1,0:T(8,128)(2,1)S(1)} copy(bf16[23,90,1024]{2,0,1:T(8,128)(2,1)} %param.1) | data formatting | bytes 8478720 | tf_op args[0]
  12.1 0.0 copy-start.1
  12.1 13.2 %collective-permute-done = bf16[23,10,1024]{2,0,1:T(8,128)(2,1)S(1)} collective-permute-done((bf16[23,10,1024]{2,0,1:T(8,128)(2,1)S(1)}, bf16[23,10,1024]{2,0,1:T(8,128)(2,1)S(1)}, u32[]{:S(2)}, u32[]{:S(2)}) %collective-permute-start) | collective-permute-done | bytes 471072 | tf_op jit(solution)/shard_map/ppermute | solution.py:17
  25.3 0.3 copy.6
  25.6 1.9 %collective-permute-done.1 = bf16[23,10,1024]{2,0,1:T(8,128)(2,1)S(1)} collective-permute-done((bf16[23,10,1024]{2,0,1:T(8,128)(2,1)S(1)}, bf16[23,10,1024]{2,0,1:T(8,128)(2,1)S(1)}, u32[]{:S(2)}, u32[]{:S(2)}) %collective-permute-start.1) | collective-permute-done | bytes 471072 | tf_op jit(solution)/shard_map/ppermute | solution.py:19
  27.5 0.3 copy.8
  27.8 2.5 %pad_maximum_fusion = bf16[23,110,1024]{2,1,0:T(8,128)(2,1)S(1)} fusion(bf16[23,10,1024]{2,1,0:T(8,128)(2,1)S(1)} %copy.8, bf16[23,90,1024]{2,1,0:T(8,128)(2,1)S(1)} %copy.7, bf16[23,10,1024]{2,1,0:T(8,128)(2,1)S(1)} %copy.6), kind=kLoop, calls=%fused_computation.10 | loop fusion | flops 15544320 | bytes 10362880 | tf_op jit(solution)/shard_map/concatenate | solution.py:15
  30.3 1.2 fusion.8
  31.5 0.1 collective-permute-start.2
  31.6 1.7 %collective-permute-start.3 = (bf16[15,110,1024]{2,1,0:T(8,128)(2,1)S(1)}, bf16[15,110,1024]{2,1,0:T(8,128)(2,1)S(1)}, u32[]{:S(2)}, u32[]{:S(2)}) collective-permute-start(bf16[15,110,1024]{2,1,0:T(8,128)(2,1)S(1)} %get-tuple-element.6), channel_id=1, source_target_pairs={{1,0},{2,1},{3,2},{0,3},{5,4},{6,5},{7,6},{4,7},{9,8},{10,9},{11,1... | collective-permute-start | bytes 10137608 | tf_op jit(solution)/shard_map/ppermute | solution.py:19
  33.3 73.3 %collective-permute-done.2 = bf16[15,110,1024]{2,1,0:T(8,128)(2,1)} collective-permute-done((bf16[15,110,1024]{2,1,0:T(8,128)(2,1)S(1)}, bf16[15,110,1024]{2,1,0:T(8,128)(2,1)}, u32[]{:S(2)}, u32[]{:S(2)}) %collective-permute-start.2) | collective-permute-done | bytes 3379232 | tf_op jit(solution)/shard_map/ppermute | solution.py:17
  106.6 0.7 collective-permute-done.3
  107.3 0.0 copy-done.1
  107.3 0.0 copy-start.2
  107.3 1.8 %copy-done.2 = bf16[15,110,1024]{2,1,0:T(8,128)(2,1)} copy-done((bf16[15,110,1024]{2,1,0:T(8,128)(2,1)}, bf16[15,110,1024]{2,1,0:T(8,128)(2,1)S(1)}, u32[]{:S(2)}) %copy-start.2) | copy-done | bytes 3379224
  109.1 11.3 %fusion.7 = f32[53,110,1024]{2,1,0:T(8,128)} fusion(bf16[15,110,1024]{2,1,0:T(8,128)(2,1)S(1)} %collective-permute-done.3, bf16[23,10,1024]{2,1,0:T(8,128)(2,1)S(1)} %copy.8, bf16[23,90,1024]{2,1,0:T(8,128)(2,1)S(1)} %copy.7, bf16[23,10,1024]{2,1,0:T(8,128)(2,1)S(1)} %copy.6, bf16[15,110,1024]{2,1,0:T(8,128)(2,1)} %collective-permute-done.2), kind=kOutput, calls=%fused_computation.11 | output fusion | flops 370135040 | bytes 35819520 | tf_op jit(solution)/shard_map/jit(cumsum)/reduce_window_sum | solution.py:28
  120.4 0.0 copy-start
  120.4 14.7 %maximum_convert_fusion = f32[53,110,1024]{2,1,0:T(8,128)} fusion(bf16[15,110,1024]{2,1,0:T(8,128)(2,1)} %copy-done.2, bf16[23,10,1024]{2,1,0:T(8,128)(2,1)S(1)} %copy.8, bf16[23,90,1024]{2,1,0:T(8,128)(2,1)} %copy-done.1, bf16[23,10,1024]{2,1,0:T(8,128)(2,1)S(1)} %copy.6, bf16[15,110,1024]{2,1,0:T(8,128)(2,1)} %collective-permute-done.2), kind=kLoop, calls=%fused_computation.1 | loop fusion | flops 59699200 | bytes 35819520 | tf_op jit(solution)/shard_map/convert_element_type | solution.py:39
  135.1 5.6 %copy-done = f32[53,110,1024]{2,1,0:T(8,128)S(1)} copy-done((f32[53,110,1024]{2,1,0:T(8,128)S(1)}, f32[53,110,1024]{2,1,0:T(8,128)}, u32[]{:S(2)}) %copy-start) | copy-done | bytes 23879704
  140.7 11.8 %fusion.4 = f32[23,110,1024]{2,1,0:T(8,128)} fusion(f32[53,110,1024]{2,1,0:T(8,128)S(1)} %copy-done, f32[53,110,1024]{2,1,0:T(8,128)} %maximum_convert_fusion), kind=kLoop, calls=%fused_computation.7 | loop fusion | flops 7772160 | bytes 55590912 | tf_op jit(solution)/shard_map/sub | solution.py:41
  152.4 10.7 %fusion = f32[23,110,1024]{2,0,1:T(8,128)S(1)} fusion(f32[23,110,1024]{2,1,0:T(8,128)} %fusion.4), kind=kOutput, calls=%fused_computation.3 | output fusion | flops 282388480 | bytes 20725760 | tf_op jit(solution)/shard_map/jit(cumsum)/reduce_window_sum | solution.py:28
  163.1 4.6 %fusion.6 = f32[23,90,1024]{2,0,1:T(8,128)} fusion(f32[23,110,1024]{2,0,1:T(8,128)S(1)} %fusion), kind=kLoop, calls=%fused_computation.9 | loop fusion | flops 4239360 | bytes 28139520 | tf_op jit(solution)/shard_map/div | solution.py:33
Async XLA Ops:
  1.2 24.1 %collective-permute-start = (bf16[23,10,1024]{2,0,1:T(8,128)(2,1)S(1)}, bf16[23,10,1024]{2,0,1:T(8,128)(2,1)S(1)}, u32[]{:S(2)}, u32[]{:S(2)}) collective-permute-start(bf16[23,10,1024]{2,0,1:T(8,128)(2,1)S(1)} %get-tuple-element.7), channel_id=1, source_target_pairs={{0,4},{4,8},{8,12},{12,16},{16,20},{20,24},{24,28},{28,0},{1,5},{5... | collective-permute-start | bytes 1413128 | tf_op jit(solution)/shard_map/ppermute | solution.py:17
  4.3 23.2 %collective-permute-start.1 = (bf16[23,10,1024]{2,0,1:T(8,128)(2,1)S(1)}, bf16[23,10,1024]{2,0,1:T(8,128)(2,1)S(1)}, u32[]{:S(2)}, u32[]{:S(2)}) collective-permute-start(bf16[23,10,1024]{2,0,1:T(8,128)(2,1)S(1)} %get-tuple-element.8), channel_id=1, source_target_pairs={{4,0},{8,4},{12,8},{16,12},{20,16},{24,20},{28,24},{0,28},{5,1},{9... | collective-permute-start | bytes 1413128 | tf_op jit(solution)/shard_map/ppermute | solution.py:19
  12.1 95.2 %copy-start.1 = (bf16[23,90,1024]{2,1,0:T(8,128)(2,1)}, bf16[23,90,1024]{2,1,0:T(8,128)(2,1)S(1)}, u32[]{:S(2)}) copy-start(bf16[23,90,1024]{2,1,0:T(8,128)(2,1)S(1)} %copy.7) | copy-start | bytes 12718084
  31.5 75.1 %collective-permute-start.2 = (bf16[15,110,1024]{2,1,0:T(8,128)(2,1)S(1)}, bf16[15,110,1024]{2,1,0:T(8,128)(2,1)}, u32[]{:S(2)}, u32[]{:S(2)}) collective-permute-start(bf16[15,110,1024]{2,1,0:T(8,128)(2,1)S(1)} %get-tuple-element.5), channel_id=1, source_target_pairs={{0,1},{1,2},{2,3},{3,0},{4,5},{5,6},{6,7},{7,4},{8,9},{9,10},{10,1... | collective-permute-start | bytes 10137608 | tf_op jit(solution)/shard_map/ppermute | solution.py:17
  31.6 75.7 %collective-permute-start.3 = (bf16[15,110,1024]{2,1,0:T(8,128)(2,1)S(1)}, bf16[15,110,1024]{2,1,0:T(8,128)(2,1)S(1)}, u32[]{:S(2)}, u32[]{:S(2)}) collective-permute-start(bf16[15,110,1024]{2,1,0:T(8,128)(2,1)S(1)} %get-tuple-element.6), channel_id=1, source_target_pairs={{1,0},{2,1},{3,2},{0,3},{5,4},{6,5},{7,6},{4,7},{9,8},{10,9},{11,1... | collective-permute-start | bytes 10137608 | tf_op jit(solution)/shard_map/ppermute | solution.py:19
  107.3 1.8 %copy-start.2 = (bf16[15,110,1024]{2,1,0:T(8,128)(2,1)}, bf16[15,110,1024]{2,1,0:T(8,128)(2,1)S(1)}, u32[]{:S(2)}) copy-start(bf16[15,110,1024]{2,1,0:T(8,128)(2,1)S(1)} %collective-permute-done.3) | copy-start | bytes 10137604
  120.4 20.3 %copy-start = (f32[53,110,1024]{2,1,0:T(8,128)S(1)}, f32[53,110,1024]{2,1,0:T(8,128)}, u32[]{:S(2)}) copy-start(f32[53,110,1024]{2,1,0:T(8,128)} %fusion.7) | copy-start | bytes 71639040
where the time goes:
time: 168 us
  waiting for transfers between devices  89.1 us (53%)
  other arithmetic  55.6 us (33%)
  local copies, waits for them, and re-layouts  15.1 us (9%)
  starting transfers between devices  7.94 us (5%)
    ppermute x2, waiting for transfers between devices, extended_2(): lax.ppermute(tail, axis, [(i, (i + 1) % count) for i in range(count)])  86.5 us
    another operation x2, other arithmetic, running(): total = jnp.cumsum(values, axis=dim)  21.9 us
    convert_element_type x1, other arithmetic, local(): values = extended.astype(jnp.float32)  14.7 us
    unnamed x7, local copies, waits for them, and re-layouts  12.1 us
    sub x1, other arithmetic, local(): anomaly = values[DAY_HALF:values.shape[0] - DAY_HALF] - clim  11.8 us
    ppermute x2, starting transfers between devices, extended_2(): lax.ppermute(head, axis, [((i + 1) % count, i) for i in range(count)])  4.84 us
    div x1, other arithmetic, running(): return (upper - lower) / (2.0 * half + 1.0)  4.63 us
  transfers between devices with their start and end apart: 4, of which 4 were waited for; matrix products, arithmetic and copies ran while one was open for 3% of the time, Pallas kernels for 0%

commit v1 on v0

v1 whole, which is shorter than its diff:
```python
import functools

import jax
import jax.numpy as jnp
from jax import lax
from jax.experimental import pallas as pl
from jax.experimental.pallas import tpu as pltpu
from jax.sharding import PartitionSpec as P

DAY_HALF = 15
LON_HALF = 10
ROWS = 8
MESH = pl.DeviceIdType.MESH


def pieces(lo, hi, size):
    return [(at, min(size, hi - at)) for at in range(lo, hi, size)]


def plan(lons):
    half = LON_HALF
    left = pieces(0, half, half // 2)
    right = pieces(lons - half, lons, half // 2)
    edges = [piece for pair in zip(left, right) for piece in pair]
    middle = pieces(half, lons - half, half)
    at, size = middle.pop()
    middle += pieces(at, at + size, half // 2)
    return edges, middle


def band(days, rows, shift):
    day = lax.broadcasted_iota(jnp.int32, (days, rows), 0)
    other = lax.broadcasted_iota(jnp.int32, (days, rows), 1) + shift
    away = jnp.abs(day - other)
    weight = jnp.where(away <= DAY_HALF, -1.0, 0.0)
    if shift == 0:
        weight = jnp.where(away == 0, 2.0 * DAY_HALF, weight)
    return weight.astype(jnp.bfloat16)


def kernel(
    counts, x, out, own, before, after, anomaly,
    own_sem, day_send, day_recv, lon_send, lon_recv,
):
    lons, days, cols = x.shape
    half = LON_HALF
    tail = days - before.shape[1]
    head = after.shape[1]
    day_count, lon_count = counts
    day, lon = lax.axis_index("day"), lax.axis_index("lon")
    day_next = lax.rem(day + 1, day_count)
    day_back = lax.rem(day + day_count - 1, day_count)
    lon_next = lax.rem(lon + 1, lon_count)
    lon_back = lax.rem(lon + lon_count - 1, lon_count)
    edges, middle = plan(lons)
    order = edges + middle

    loads = []
    for n, (at, size) in enumerate(order):
        loads.append(
            pltpu.make_async_copy(
                x.at[pl.ds(at, size)], own.at[pl.ds(at, size)], own_sem.at[n]
            )
        )
        loads[-1].start()

    barrier = pltpu.get_barrier_semaphore()
    for axis, peer in (
        ("day", day_next), ("day", day_back), ("lon", lon_next), ("lon", lon_back),
    ):
        pl.semaphore_signal(
            barrier, inc=1, device_id={axis: peer}, device_id_type=MESH
        )
    pl.semaphore_wait(barrier, 4)

    swaps = []
    for n, (at, size) in enumerate(order):
        up = pltpu.make_async_remote_copy(
            src_ref=x.at[pl.ds(at, size), pl.ds(tail, days - tail)],
            dst_ref=before.at[pl.ds(at, size)],
            send_sem=day_send.at[0, n],
            recv_sem=day_recv.at[0, n],
            device_id={"day": day_next},
            device_id_type=MESH,
        )
        down = pltpu.make_async_remote_copy(
            src_ref=x.at[pl.ds(at, size), pl.ds(0, head)],
            dst_ref=after.at[pl.ds(at, size)],
            send_sem=day_send.at[1, n],
            recv_sem=day_recv.at[1, n],
            device_id={"day": day_back},
            device_id_type=MESH,
        )
        up.start()
        down.start()
        swaps.append((up, down))

    own_band = band(days, days, 0)
    before_band = band(days, days - tail, tail - days)
    after_band = band(days, head, days)

    def dot(weight, values):
        return jnp.dot(weight, values, preferred_element_type=jnp.float32)

    def daily(n):
        at, size = order[n]
        loads[n].wait()
        for copy in swaps[n]:
            copy.wait_recv()

        @pl.loop(at, at + size)
        def _(l):
            anomaly[l + half] = (
                dot(own_band, own[l])
                + dot(before_band, before[l])
                + dot(after_band, after[l])
            )

    def edge(n):
        at, size = order[n]
        low = at < half
        place = at + lons + half if low else at - lons + half
        side = 0 if low else 1
        copy = pltpu.make_async_remote_copy(
            src_ref=anomaly.at[pl.ds(at + half, size)],
            dst_ref=anomaly.at[pl.ds(place, size)],
            send_sem=lon_send.at[side, n],
            recv_sem=lon_recv.at[side, n],
            device_id={"lon": lon_back if low else lon_next},
            device_id_type=MESH,
        )
        copy.start()
        return copy

    shifts = []
    for n in range(len(edges)):
        daily(n)
        shifts.append(edge(n))

    scale = 1.0 / ((2 * DAY_HALF + 1) * (2 * half + 1))
    width = 2 * half + 1

    def up_to(lo, hi, total):
        def step(l, total):
            total = total + (anomaly[l + width - 1] - anomaly[l - 1])
            out[l] = total * scale
            return total

        return lax.fori_loop(lo, hi, step, total)

    total = None
    done = half
    for n in range(len(edges), len(order)):
        daily(n)
        ready = sum(order[n]) - half
        if n == len(order) - 1:
            ready = lons - half
        if ready <= half:
            continue
        if total is None:
            total = lax.fori_loop(
                half, half + width, lambda l, t: t + anomaly[l], jnp.zeros((days, cols), jnp.float32)
            )
            out[half] = total * scale
            first = total
            done = half + 1
        total = up_to(done, ready, total)
        done = ready
    for copy in shifts:
        copy.wait_recv()
    up_to(done, lons, total)

    def back(step, total):
        l = half - 1 - step
        total = total + (anomaly[l] - anomaly[l + width])
        out[l] = total * scale
        return total

    lax.fori_loop(0, half, back, first)

    for pair in swaps:
        for copy in pair:
            copy.wait_send()
    for copy in shifts:
        copy.wait_send()


def local(counts, field):
    days, lons, cols = field.shape
    x = jnp.transpose(field, (1, 0, 2))
    tail = (days - DAY_HALF) // ROWS * ROWS
    head = min(days, (DAY_HALF + ROWS - 1) // ROWS * ROWS)
    edges, middle = plan(lons)
    steps = len(edges) + len(middle)
    y = pl.pallas_call(
        functools.partial(kernel, counts),
        out_shape=pltpu.VMEM((lons, days, cols), jnp.float32),
        in_specs=[pl.BlockSpec(memory_space=pltpu.HBM)],
        out_specs=pl.BlockSpec(memory_space=pltpu.VMEM),
        scratch_shapes=[
            pltpu.VMEM((lons, days, cols), jnp.bfloat16),
            pltpu.VMEM((lons, days - tail, cols), jnp.bfloat16),
            pltpu.VMEM((lons, head, cols), jnp.bfloat16),
            pltpu.VMEM((lons + 2 * LON_HALF, days, cols), jnp.float32),
            pltpu.SemaphoreType.DMA((steps,)),
            pltpu.SemaphoreType.DMA((2, steps)),
            pltpu.SemaphoreType.DMA((2, steps)),
            pltpu.SemaphoreType.DMA((2, len(edges))),
            pltpu.SemaphoreType.DMA((2, len(edges))),
        ],
        compiler_params=pltpu.CompilerParams(
            collective_id=0, has_side_effects=True, vmem_limit_bytes=50 * 1024 * 1024
        ),
    )(x)
    return jnp.transpose(y, (1, 0, 2))


def solution(mesh):
    return jax.shard_map(
        functools.partial(local, (mesh.shape["day"], mesh.shape["lon"])),
        mesh=mesh,
        in_specs=(P("day", "lon", None),),
        out_specs=P("day", "lon", None),
        check_vma=False,
    )
```

time: 168 us -> 76.7 us (0.46)
  waiting for transfers between devices: 89.1 us -> 0 us
  Pallas kernels: 0 us -> 72.5 us
  other arithmetic: 55.6 us -> 0 us
  local copies, waits for them, and re-layouts: 15.1 us -> 3.55 us
  starting transfers between devices: 7.94 us -> 0 us
    ppermute x4 -> x0, waiting for transfers between devices: 89.1 us -> none  [the longest x2 86.5 us: extended_2(): lax.ppermute(tail, axis, [(i, (i + 1) % count) for i in range(count)])]
    pallas_call x0 -> x1, Pallas kernels: none -> 72.5 us  [local(): pl.pallas_call(functools.partial(kernel, counts), out_shape=pltpu.VMEM((l...]
    another operation x2 -> x0, other arithmetic: 21.9 us -> none  [running(): total = jnp.cumsum(values, axis=dim)]
    convert_element_type x1 -> x0, other arithmetic: 14.7 us -> none  [local(): values = extended.astype(jnp.float32)]
    sub x1 -> x0, other arithmetic: 11.8 us -> none  [local(): anomaly = values[DAY_HALF:values.shape[0] - DAY_HALF] - clim]
    unnamed x7 -> x1, local copies, waits for them, and re-layouts: 12.1 us -> 3.55 us
    ppermute x4 -> x0, starting transfers between devices: 7.94 us -> none  [the longest x2 4.84 us: extended_2(): lax.ppermute(head, axis, [((i + 1) % count, i) for i in range(count)])]
    div x1 -> x0, other arithmetic: 4.63 us -> none  [running(): return (upper - lower) / (2.0 * half + 1.0)]
  transfers between devices with their start and end apart: 4 -> 0, of which waited for: 4 -> 0; matrix products, arithmetic and copies ran while one was open for 3% -> 0% of each run, Pallas kernels for 0% -> 0%
where the time goes in v1:
time: 76.7 us; the launch traced here: 76.1 us
  Pallas kernels  72.5 us (95%)
  local copies, waits for them, and re-layouts  3.55 us (5%)
    pallas_call x1, Pallas kernels, local(): pl.pallas_call(functools.partial(kernel, counts), out_shape=pltpu.VMEM((l...  72.5 us
    unnamed x1, local copies, waits for them, and re-layouts  3.55 us

profile of v1, /device:TPU:0, one launch (start us, length us, event | category | flops | bytes accessed | tf_op | source)
XLA Modules:
  0.0 76.1 jit_solution(13856662500418159490)
XLA Ops:
  0.0 72.5 %shard_map.17 = f32[90,23,1024]{2,1,0:T(8,128)S(1)} custom-call(bf16[90,23,1024]{2,1,0:T(8,128)(2,1)} %bitcast.3), custom_call_target="tpu_custom_call" | custom-call | tf_op jit(solution)/shard_map/pallas_call | solution.py:195
  72.6 3.6 %copy.3 = f32[23,90,1024]{2,0,1:T(8,128)} copy(f32[23,90,1024]{2,0,1:T(8,128)S(1)} %bitcast.2) | data formatting | bytes 16957440

commit v2 on v1

v2 whole, which is shorter than its diff:
```python
import functools

import jax
import jax.numpy as jnp
from jax import lax
from jax.experimental import pallas as pl
from jax.experimental.pallas import tpu as pltpu
from jax.sharding import PartitionSpec as P

DAY_HALF = 15
LON_HALF = 10
ROWS = 8
PAD = 24
LEAD = 3
MESH = pl.DeviceIdType.MESH


def plan(lons):
    group = DAY_HALF % ROWS + 1
    depth = -(-LON_HALF // group) * group
    left = [(at, group) for at in range(0, depth, group)]
    right = [(lons - at - group, group) for at in range(0, depth, group)]
    edges = [piece for pair in zip(left, right) for piece in pair]
    middle = [
        (at, min(group, lons - depth - at)) for at in range(depth, lons - depth, group)
    ]
    return edges, middle


def grid(rows, cols):
    return (
        lax.broadcasted_iota(jnp.int32, (rows, cols), 0),
        lax.broadcasted_iota(jnp.int32, (rows, cols), 1),
    )


def ones(condition):
    return jnp.where(condition, 1.0, 0.0).astype(jnp.bfloat16)


def band(days, rows, shift):
    day, other = grid(days, rows)
    away = jnp.abs(day - other - shift)
    weight = jnp.where(away <= DAY_HALF, -1.0, 0.0)
    if shift == 0:
        weight = jnp.where(away == 0, 2.0 * DAY_HALF, weight)
    return weight.astype(jnp.bfloat16)


def stacked(days, shift, extra):
    row, other = grid(2 * PAD, 2 * ROWS)
    low = (row < days) & (other < DAY_HALF) & (jnp.abs(row - other - shift) <= DAY_HALF)
    away = jnp.abs(row - PAD - (ROWS + extra) - shift)
    high = (row >= PAD) & (row < PAD + days) & (other == DAY_HALF) & (away <= DAY_HALF)
    return jnp.where(low | high, -1.0, 0.0).astype(jnp.bfloat16)


def kernel(
    counts, x, out, own, before, after, rest_before, rest_after, pack_up, pack_down,
    anomaly, own_sem, day_send, day_recv, lon_send, lon_recv,
):
    lons, days, cols = x.shape
    half = LON_HALF
    tail = days - DAY_HALF
    part = DAY_HALF - ROWS
    group = part + 1
    day_count, lon_count = counts
    day, lon = lax.axis_index("day"), lax.axis_index("lon")
    day_next = lax.rem(day + 1, day_count)
    day_back = lax.rem(day + day_count - 1, day_count)
    lon_next = lax.rem(lon + 1, lon_count)
    lon_back = lax.rem(lon + lon_count - 1, lon_count)
    edges, middle = plan(lons)
    order = edges + middle

    loads = []
    for n, (at, size) in enumerate(order):
        loads.append(
            pltpu.make_async_copy(
                x.at[pl.ds(at, size)], own.at[pl.ds(at, size)], own_sem.at[n]
            )
        )
        loads[-1].start()

    barrier = pltpu.get_barrier_semaphore()
    for axis, peer in (
        ("day", day_next), ("day", day_back), ("lon", lon_next), ("lon", lon_back),
    ):
        pl.semaphore_signal(
            barrier, inc=1, device_id={axis: peer}, device_id_type=MESH
        )
    pl.semaphore_wait(barrier, 4)

    swaps = [[] for _ in order]

    def swap(n, kind, up_src, up_dst, down_src, down_dst):
        for way, src, dst, peer in (
            (0, up_src, up_dst, day_next), (1, down_src, down_dst, day_back),
        ):
            copy = pltpu.make_async_remote_copy(
                src_ref=src,
                dst_ref=dst,
                send_sem=day_send.at[kind, way, n],
                recv_sem=day_recv.at[kind, way, n],
                device_id={"day": peer},
                device_id_type=MESH,
            )
            copy.start()
            swaps[n].append(copy)

    def whole(n):
        at, size = order[n]
        if size == group:
            rows = pl.ds(at, size)
            swap(
                n, 0,
                x.at[rows, pl.ds(tail, ROWS)], before.at[rows, pl.ds(0, ROWS)],
                x.at[rows, pl.ds(0, ROWS)], after.at[rows, pl.ds(0, ROWS)],
            )
        else:
            rows = pl.ds(at, size)
            swap(
                n, 0,
                x.at[rows, pl.ds(tail, DAY_HALF)], rest_before,
                x.at[rows, pl.ds(0, 2 * ROWS)], rest_after,
            )

    row, col = grid(2 * ROWS, days)
    first_day = jnp.where(row < ROWS, tail + ROWS, ROWS)
    place = jnp.where(row < ROWS, row, row - ROWS)
    keep = ones((place < part) & (col == first_day + place))

    def dot(weight, values):
        return jnp.dot(weight, values, preferred_element_type=jnp.float32)

    def pack(n):
        at, size = order[n]
        loads[n].wait()
        if size < group:
            return

        @pl.loop(0, part)
        def _(i):
            ride = ones((place == part) & (col == first_day + i))
            tile = dot(keep, own[at + i]) + dot(ride, own[at + part])
            tile = tile.astype(jnp.bfloat16)
            pack_up[at + i] = tile[:ROWS]
            pack_down[at + i] = tile[ROWS:]

    def packed(n):
        at, size = order[n]
        if size == group:
            rows = pl.ds(at, part)
            swap(
                n, 1,
                pack_up.at[rows], before.at[rows, pl.ds(ROWS, ROWS)],
                pack_down.at[rows], after.at[rows, pl.ds(ROWS, ROWS)],
            )

    own_band = band(days, days, 0)
    before_band = band(days, DAY_HALF, -DAY_HALF)
    after_band = band(days, 2 * ROWS, days)
    before_top = band(days, ROWS, -DAY_HALF)
    after_top = band(days, ROWS, days)

    def daily(n):
        at, size = order[n]
        for copy in swaps[n]:
            copy.wait_recv()
        if size < group:
            for i in range(size):
                anomaly[at + i + half] = (
                    dot(own_band, own[at + i])
                    + dot(before_band, rest_before[i])
                    + dot(after_band, rest_after[i])
                )
            return

        last = at + part
        anomaly[last + half] = (
            dot(own_band, own[last])
            + dot(before_top, before[last, pl.ds(0, ROWS)])
            + dot(after_top, after[last, pl.ds(0, ROWS)])
        )

        @pl.loop(0, part)
        def _(i):
            l = at + i
            both = dot(stacked(days, -DAY_HALF, i), before[l]) + dot(
                stacked(days, days, i), after[l]
            )
            anomaly[l + half] = dot(own_band, own[l]) + both[:days]
            anomaly[last + half] = anomaly[last + half] + both[PAD : PAD + days]

    def edge(n):
        at, size = order[n]
        low = n % 2 == 0
        if low:
            size = min(size, half - at)
            place = at + lons + half
        else:
            end = at + size
            at = max(at, lons - half)
            size = end - at
            place = at - lons + half
        side = 0 if low else 1
        copy = pltpu.make_async_remote_copy(
            src_ref=anomaly.at[pl.ds(at + half, size)],
            dst_ref=anomaly.at[pl.ds(place, size)],
            send_sem=lon_send.at[side, n],
            recv_sem=lon_recv.at[side, n],
            device_id={"lon": lon_back if low else lon_next},
            device_id_type=MESH,
        )
        copy.start()
        return copy

    for n in range(LEAD):
        whole(n)
    for n in range(len(order)):
        pack(n)
        if n > 0:
            packed(n - 1)
        if n + LEAD < len(order):
            whole(n + LEAD)

    packed(len(order) - 1)

    shifts = []
    for n in range(len(edges)):
        daily(n)
        if n > 0:
            shifts.append(edge(n - 1))

    scale = 1.0 / ((2 * DAY_HALF + 1) * (2 * half + 1))
    width = 2 * half + 1

    def up_to(lo, hi, total):
        def step(l, total):
            total = total + (anomaly[l + width - 1] - anomaly[l - 1])
            out[l] = total * scale
            return total

        return lax.fori_loop(lo, hi, step, total)

    def back(step, total):
        l = half - 1 - step
        total = total + (anomaly[l] - anomaly[l + width])
        out[l] = total * scale
        return total

    total = None
    done = half
    for n in range(len(edges), len(order)):
        end = n == len(order) - 1
        if end and total is not None:
            for copy in shifts:
                copy.wait_recv()
            lax.fori_loop(0, half, back, first)
        daily(n)
        if n == len(edges):
            shifts.append(edge(n - 1))
        ready = lons - half if end else sum(order[n]) - half
        if ready <= half:
            continue
        fresh = total is None
        if fresh:
            total = lax.fori_loop(
                half,
                half + width,
                lambda l, t: t + anomaly[l],
                jnp.zeros((days, cols), jnp.float32),
            )
            out[half] = total * scale
            first = total
            done = half + 1
        total = up_to(done, ready, total)
        done = ready
    up_to(done, lons, total)

    for copies in swaps:
        for copy in copies:
            copy.wait_send()
    for copy in shifts:
        copy.wait_send()


def local(counts, field):
    days, lons, cols = field.shape
    x = jnp.transpose(field, (1, 0, 2))
    edges, middle = plan(lons)
    steps = len(edges) + len(middle)
    rest = middle[-1][1]
    y = pl.pallas_call(
        functools.partial(kernel, counts),
        out_shape=pltpu.VMEM((lons, days, cols), jnp.float32),
        in_specs=[pl.BlockSpec(memory_space=pltpu.HBM)],
        out_specs=pl.BlockSpec(memory_space=pltpu.VMEM),
        scratch_shapes=[
            pltpu.VMEM((lons, days, cols), jnp.bfloat16),
            pltpu.VMEM((lons, 2 * ROWS, cols), jnp.bfloat16),
            pltpu.VMEM((lons, 2 * ROWS, cols), jnp.bfloat16),
            pltpu.VMEM((rest, DAY_HALF, cols), jnp.bfloat16),
            pltpu.VMEM((rest, 2 * ROWS, cols), jnp.bfloat16),
            pltpu.VMEM((lons, ROWS, cols), jnp.bfloat16),
            pltpu.VMEM((lons, ROWS, cols), jnp.bfloat16),
            pltpu.VMEM((lons + 2 * LON_HALF, days, cols), jnp.float32),
            pltpu.SemaphoreType.DMA((steps,)),
            pltpu.SemaphoreType.DMA((2, 2, steps)),
            pltpu.SemaphoreType.DMA((2, 2, steps)),
            pltpu.SemaphoreType.DMA((2, len(edges))),
            pltpu.SemaphoreType.DMA((2, len(edges))),
        ],
        compiler_params=pltpu.CompilerParams(
            collective_id=0, has_side_effects=True, vmem_limit_bytes=50 * 1024 * 1024
        ),
    )(x)
    return jnp.transpose(y, (1, 0, 2))


def solution(mesh):
    return jax.shard_map(
        functools.partial(local, (mesh.shape["day"], mesh.shape["lon"])),
        mesh=mesh,
        in_specs=(P("day", "lon", None),),
        out_specs=P("day", "lon", None),
        check_vma=False,
    )
```

time: 76.7 us -> 76 us (level)
  the two profiles are of different devices: /device:TPU:0 before, /device:TPU:29 now
where the time goes in v2:
time: 76 us; the launch traced here: 75.9 us
  Pallas kernels  72.3 us (95%)
  local copies, waits for them, and re-layouts  3.55 us (5%)
    pallas_call x1, Pallas kernels, local(): pl.pallas_call(functools.partial(kernel, counts), out_shape=pltpu.VMEM((l...  72.3 us
    unnamed x1, local copies, waits for them, and re-layouts  3.55 us

profile of v2, /device:TPU:29, one launch (start us, length us, event | category | flops | bytes accessed | tf_op | source)
XLA Modules:
  0.0 75.9 jit_solution(2260970789572880864)
XLA Ops:
  0.0 72.3 %shard_map.17 = f32[90,23,1024]{2,1,0:T(8,128)S(1)} custom-call(bf16[90,23,1024]{2,1,0:T(8,128)(2,1)} %bitcast.3), custom_call_target="tpu_custom_call" | custom-call | tf_op jit(solution)/shard_map/pallas_call | solution.py:294
  72.4 3.6 %copy.3 = f32[23,90,1024]{2,0,1:T(8,128)} copy(f32[23,90,1024]{2,0,1:T(8,128)S(1)} %bitcast.2) | data formatting | bytes 16957440

commit v3 on v2

--- a/solution.py
+++ b/solution.py
@@ -215,22 +215,29 @@
         copy.start()
         return copy
 
+    steps = len(order)
     for n in range(LEAD):
         whole(n)
-    for n in range(len(order)):
+    for n in range(LEAD):
         pack(n)
         if n > 0:
             packed(n - 1)
-        if n + LEAD < len(order):
+
+    shifts = []
+
+    def advance(n):
+        daily(n)
+        if n + LEAD < steps:
+            pack(n + LEAD)
+        if n < len(edges):
+            shifts.append(edge(n))
+        if n + LEAD - 1 < steps:
+            packed(n + LEAD - 1)
+        if n + LEAD < steps:
             whole(n + LEAD)
 
-    packed(len(order) - 1)
-
-    shifts = []
     for n in range(len(edges)):
-        daily(n)
-        if n > 0:
-            shifts.append(edge(n - 1))
+        advance(n)
 
     scale = 1.0 / ((2 * DAY_HALF + 1) * (2 * half + 1))
     width = 2 * half + 1
@@ -251,15 +258,13 @@
 
     total = None
     done = half
-    for n in range(len(edges), len(order)):
-        end = n == len(order) - 1
+    for n in range(len(edges), steps):
+        end = n == steps - 1
         if end and total is not None:
             for copy in shifts:
                 copy.wait_recv()
             lax.fori_loop(0, half, back, first)
-        daily(n)
-        if n == len(edges):
-            shifts.append(edge(n - 1))
+        advance(n)
         ready = lons - half if end else sum(order[n]) - half
         if ready <= half:
             continue

time: 76 us -> 75.6 us (level)
  the two profiles are of different devices: /device:TPU:29 before, /device:TPU:0 now
where the time goes in v3:
time: 75.6 us; the launch traced here: 75.5 us
  Pallas kernels  71.9 us (95%)
  local copies, waits for them, and re-layouts  3.55 us (5%)
    pallas_call x1, Pallas kernels, local(): pl.pallas_call(functools.partial(kernel, counts), out_shape=pltpu.VMEM((l...  71.9 us
    unnamed x1, local copies, waits for them, and re-layouts  3.55 us

profile of v3, /device:TPU:0, one launch (start us, length us, event | category | flops | bytes accessed | tf_op | source)
XLA Modules:
  0.0 75.5 jit_solution(11601294065500149316)
XLA Ops:
  0.0 71.9 %shard_map.17 = f32[90,23,1024]{2,1,0:T(8,128)S(1)} custom-call(bf16[90,23,1024]{2,1,0:T(8,128)(2,1)} %bitcast.3), custom_call_target="tpu_custom_call" | custom-call | tf_op jit(solution)/shard_map/pallas_call | solution.py:299
  71.9 3.6 %copy.3 = f32[23,90,1024]{2,0,1:T(8,128)} copy(f32[23,90,1024]{2,0,1:T(8,128)S(1)} %bitcast.2) | data formatting | bytes 16957440

commit v4 on v3

--- a/solution.py
+++ b/solution.py
@@ -58,6 +58,7 @@
 def kernel(
     counts, x, out, own, before, after, rest_before, rest_after, pack_up, pack_down,
     anomaly, own_sem, day_send, day_recv, lon_send, lon_recv,
+    day_ready, lon_ready,
 ):
     lons, days, cols = x.shape
     half = LON_HALF
@@ -83,13 +84,28 @@
         loads[-1].start()
 
     barrier = pltpu.get_barrier_semaphore()
-    for axis, peer in (
-        ("day", day_next), ("day", day_back), ("lon", lon_next), ("lon", lon_back),
-    ):
-        pl.semaphore_signal(
-            barrier, inc=1, device_id={axis: peer}, device_id_type=MESH
-        )
-    pl.semaphore_wait(barrier, 4)
+    even = lax.rem(day, 2) == 0
+    odd = jnp.logical_not(even)
+
+    def tell(semaphore, axis, peers):
+        for peer in peers:
+            pl.semaphore_signal(
+                semaphore, inc=1, device_id={axis: peer}, device_id_type=MESH
+            )
+
+    @pl.when(odd)
+    def _():
+        tell(barrier, "day", (day_next, day_back))
+
+    @pl.when(even)
+    def _():
+        pl.semaphore_wait(barrier, 2)
+        tell(day_ready, "day", (day_next, day_back))
+
+    @pl.when(odd)
+    def _():
+        pl.semaphore_wait(day_ready, 2)
+        tell(barrier, "lon", (lon_next, lon_back))
 
     swaps = [[] for _ in order]
 
@@ -218,23 +234,28 @@
     steps = len(order)
     for n in range(LEAD):
         whole(n)
-    for n in range(LEAD):
+    for n in range(steps):
         pack(n)
         if n > 0:
             packed(n - 1)
-
+    packed(steps - 1)
+    for n in range(LEAD, steps):
+        whole(n)
     shifts = []
 
     def advance(n):
         daily(n)
-        if n + LEAD < steps:
-            pack(n + LEAD)
-        if n < len(edges):
-            shifts.append(edge(n))
-        if n + LEAD - 1 < steps:
-            packed(n + LEAD - 1)
-        if n + LEAD < steps:
-            whole(n + LEAD)
+        if 0 < n <= len(edges):
+            shifts.append(edge(n - 1))
+
+    @pl.when(odd)
+    def _():
+        pl.semaphore_wait(barrier, 2)
+        tell(lon_ready, "day", (day_back,))
+
+    @pl.when(even)
+    def _():
+        pl.semaphore_wait(lon_ready, 1)
 
     for n in range(len(edges)):
         advance(n)
@@ -315,6 +336,8 @@
             pltpu.SemaphoreType.DMA((2, 2, steps)),
             pltpu.SemaphoreType.DMA((2, len(edges))),
             pltpu.SemaphoreType.DMA((2, len(edges))),
+            pltpu.SemaphoreType.REGULAR,
+            pltpu.SemaphoreType.REGULAR,
         ],
         compiler_params=pltpu.CompilerParams(
             collective_id=0, has_side_effects=True, vmem_limit_bytes=50 * 1024 * 1024

time: 75.6 us -> 71.1 us (0.940)
  Pallas kernels: 71.9 us -> 67.4 us
    pallas_call x1, Pallas kernels: 71.9 us -> 67.4 us  [local(): pl.pallas_call(functools.partial(kernel, counts), out_shape=pltpu.VMEM((l...]
where the time goes in v4:
time: 71.1 us; the launch traced here: 71 us
  Pallas kernels  67.4 us (95%)
  local copies, waits for them, and re-layouts  3.55 us (5%)
    pallas_call x1, Pallas kernels, local(): pl.pallas_call(functools.partial(kernel, counts), out_shape=pltpu.VMEM((l...  67.4 us
    unnamed x1, local copies, waits for them, and re-layouts  3.55 us

profile of v4, /device:TPU:0, one launch (start us, length us, event | category | flops | bytes accessed | tf_op | source)
XLA Modules:
  0.0 71.0 jit_solution(15755348310425824195)
XLA Ops:
  0.0 67.4 %shard_map.17 = f32[90,23,1024]{2,1,0:T(8,128)S(1)} custom-call(bf16[90,23,1024]{2,1,0:T(8,128)(2,1)} %bitcast.3), custom_call_target="tpu_custom_call" | custom-call | tf_op jit(solution)/shard_map/pallas_call | solution.py:320
  67.5 3.6 %copy.3 = f32[23,90,1024]{2,0,1:T(8,128)} copy(f32[23,90,1024]{2,0,1:T(8,128)S(1)} %bitcast.2) | data formatting | bytes 16957440

commit v5 on v4

--- a/solution.py
+++ b/solution.py
@@ -11,7 +11,7 @@
 LON_HALF = 10
 ROWS = 8
 PAD = 24
-LEAD = 3
+LEAD = 2
 MESH = pl.DeviceIdType.MESH
 
 

time: 71.1 us -> 77.5 us (1.090)
  Pallas kernels: 67.4 us -> 73.8 us
    pallas_call x1, Pallas kernels: 67.4 us -> 73.8 us  [local(): pl.pallas_call(functools.partial(kernel, counts), out_shape=pltpu.VMEM((l...]
where the time goes in v5:
time: 77.5 us; the launch traced here: 77.4 us
  Pallas kernels  73.8 us (95%)
  local copies, waits for them, and re-layouts  3.55 us (5%)
    pallas_call x1, Pallas kernels, local(): pl.pallas_call(functools.partial(kernel, counts), out_shape=pltpu.VMEM((l...  73.8 us
    unnamed x1, local copies, waits for them, and re-layouts  3.55 us

profile of v5, /device:TPU:0, one launch (start us, length us, event | category | flops | bytes accessed | tf_op | source)
XLA Modules:
  0.0 77.4 jit_solution(12451564499824589299)
XLA Ops:
  0.0 73.8 %shard_map.17 = f32[90,23,1024]{2,1,0:T(8,128)S(1)} custom-call(bf16[90,23,1024]{2,1,0:T(8,128)(2,1)} %bitcast.3), custom_call_target="tpu_custom_call" | custom-call | tf_op jit(solution)/shard_map/pallas_call | solution.py:320
  73.8 3.6 %copy.3 = f32[23,90,1024]{2,0,1:T(8,128)} copy(f32[23,90,1024]{2,0,1:T(8,128)S(1)} %bitcast.2) | data formatting | bytes 16957440
